TPU v7x, 32 devices: a 4x4x1 block of a 4x4x8 slice. The times are simulated.
32 devices in a mesh: rep: 2 (over z, core), dp: 16 (over x, y).
Axes of the slice: x: 4, y: 4, z: 1, core: 2. Of those that a mesh axis runs over, the one named last changes fastest.
The devices are a block of a 4x4x8 slice.
Arguments:
- x: bfloat16 [32, 4096, 896], P(('rep', 'dp')), parts along dimension 0
- dy: bfloat16 [32, 4096, 896], P(('rep', 'dp')), parts along dimension 0
- w_gate: bfloat16 [2, 896, 2304], P(None, 'dp')
- w_up: bfloat16 [2, 896, 2304], P(None, 'dp')
- w_down: bfloat16 [2, 2304, 896], P(None, 'dp')
Outputs:
- output 1: bfloat16 [32, 4096, 896], P(('rep', 'dp')), parts along dimension 0
- output 2: bfloat16 [4, 896, 2304], P('rep', 'dp'), parts along dimension 0
- output 3: bfloat16 [4, 896, 2304], P('rep', 'dp'), parts along dimension 0
- output 4: bfloat16 [4, 2304, 896], P('rep', 'dp'), parts along dimension 0
There are 2 independent parts. A program takes and returns all parts, laid end to end along the dimension named above; an argument that names none is the same for every part.
All inputs are finite; a program needn't handle non-finite values.
Results may differ from a plain program's by a relative error of at most 0.018.
Values are sent between devices in bfloat16 or wider.
A program may use at most 768 MiB of HBM per device.

v0:
```python
import jax
import jax.numpy as jnp
from jax import lax

NAMES = ("w_gate", "w_up", "w_down")


def matmul(a, w):
    return jnp.dot(a, w, preferred_element_type=jnp.float32).astype(jnp.bfloat16)


def normed(h):
    wide = h.astype(jnp.float32)
    scale = lax.rsqrt(jnp.mean(wide**2, -1, keepdims=True) + 1e-6)
    return (wide * scale).astype(jnp.bfloat16)


def layer(h, w):
    a = normed(h)
    gate = jnp.dot(a, w["w_gate"], preferred_element_type=jnp.float32)
    up = jnp.dot(a, w["w_up"], preferred_element_type=jnp.float32)
    return h + matmul((jax.nn.silu(gate) * up).astype(jnp.bfloat16), w["w_down"])


def stack(weights, h):
    for number in range(weights["w_gate"].shape[0]):
        h = layer(h, {name: w[number] for name, w in weights.items()})
    return h


def solution(mesh):
    groups = mesh.shape["rep"]

    def step(x, dy, *weights):
        shape = x.shape
        x, dy = (t.reshape(groups, -1, *t.shape[1:]) for t in (x, dy))

        def of_a_group(x, dy):
            _, back = jax.vjp(stack, dict(zip(NAMES, weights, strict=True)), x)
            by_weights, by_x = back(dy)
            return (by_x, *(by_weights[name] for name in NAMES))

        by_x, *by_weights = jax.vmap(of_a_group)(x, dy)
        return (by_x.reshape(shape), *(t.reshape(-1, *t.shape[2:]) for t in by_weights))

    return step
```

profile of v0, /device:TPU:98, one launch (start us, length us, event | category | flops | bytes accessed | tf_op | source)
XLA Modules:
  0.0 953.2 jit_solution(16676877535315618307)
XLA Ops:
  7.2 1.9 fusion.109
  9.2 0.1 all-gather.32.cloned.1.call-start
  9.3 1.9 fusion.108
  11.2 0.1 all-gather.34.cloned.1.call-start
  11.3 1.9 fusion.107
  13.3 0.1 all-gather.36.cloned.1.call-start
  13.4 0.6 all-gather.36.cloned.1.call-update
  14.0 0.6 all-gather.40.cloned.1.call-update
  14.6 0.1 all-gather.38.cloned.1.call-start
  14.6 0.6 all-gather.38.cloned.1.call-update
  15.2 0.1 reduce-scatter.41.cloned.1.call-start
  15.3 4.6 fusion.30
  19.9 10.8 %copy.1 = bf16[1,4096,896]{1,2,0:T(8,128)(2,1)} copy(bf16[1,4096,896]{2,1,0:T(8,128)(2,1)} %param.1) | data formatting | bytes 14680064 | tf_op args[0]
  30.7 0.6 multiply_add_fusion.1
  31.3 10.8 %copy = bf16[1,4096,896]{1,2,0:T(8,128)(2,1)} copy(bf16[1,4096,896]{2,1,0:T(8,128)(2,1)} %param) | data formatting | bytes 14680064 | tf_op args[1]
  42.0 16.6 %all-gather.30.cloned.1.call-done = bf16[1,896,2304]{2,1,0:T(8,128)(2,1)} async-done(((bf16[1,56,2304]{2,1,0:T(8,128)(2,1)}), bf16[1,896,2304]{2,1,0:T(8,128)(2,1)}) %all-gather.30.cloned.1.call-update) | async-done | bytes 4128784 | tf_op jit(solution)/vmap(jvp())/squeeze | solution.py:27
  58.7 26.8 %fusion.97 = f32[4096,2304]{1,0:T(8,128)} fusion(bf16[1,896,2304]{2,1,0:T(8,128)(2,1)} %all-gather.30.cloned.1.call-done, bf16[1,4096,896]{2,1,0:T(8,128)(2,1)} %param.1, f32[4096]{0:T(1024)S(1)} %get-tuple-element.13), kind=kOutput, calls=%fused_computation.99 | convolution fusion | flops 16922443776 | bytes 49233920 | tf_op jit(solution)/vmap(jvp())/dot_general | solution.py:20
  85.5 21.1 %all-gather.32.cloned.1.call-done = bf16[1,896,2304]{2,1,0:T(8,128)(2,1)} async-done(((bf16[1,56,2304]{2,1,0:T(8,128)(2,1)}), bf16[1,896,2304]{2,1,0:T(8,128)(2,1)}) %all-gather.32.cloned.1.call-update) | async-done | bytes 4128784 | tf_op jit(solution)/vmap(jvp())/squeeze | solution.py:27
  106.6 26.7 %fusion.93 = f32[4096,2304]{1,0:T(8,128)} fusion(bf16[1,896,2304]{2,1,0:T(8,128)(2,1)} %all-gather.32.cloned.1.call-done, bf16[1,4096,896]{2,1,0:T(8,128)(2,1)} %param.1, f32[4096]{0:T(1024)S(1)} %get-tuple-element.13), kind=kOutput, calls=%fused_computation.95 | convolution fusion | flops 16922443776 | bytes 49233920 | tf_op jit(solution)/vmap(jvp())/dot_general | solution.py:21
  133.3 31.7 %fusion.26 = bf16[4096,2304]{1,0:T(8,128)(2,1)} fusion(f32[4096,2304]{1,0:T(8,128)} %fusion.93, f32[4096,2304]{1,0:T(8,128)} %fusion.97), kind=kLoop, calls=%fused_computation.45 | loop fusion | flops 56623104 | bytes 94371840
  165.0 24.6 %fusion.38 = (f32[4096]{0:T(1024)S(1)}, bf16[1,1,4096,896]{2,3,1,0:T(8,128)(2,1)}) fusion(bf16[4096,2304]{1,0:T(8,128)(2,1)} %fusion.26, bf16[1,2304,896]{2,1,0:T(8,128)(2,1)} %all-gather.34.cloned.1.call-done, bf16[1,4096,896]{1,2,0:T(8,128)(2,1)} %copy.1), kind=kOutput, calls=%fused_computation.60 | convolution fusion | flops 16929779712 | bytes 37699584 | tf_op jit(solution)/vmap(jvp())/dot_general | solution.py:9
  189.6 0.6 copy-done.2
  190.3 11.4 %all-gather.36.cloned.1.call-done = bf16[1,896,2304]{2,1,0:T(8,128)(2,1)} async-done(((bf16[1,56,2304]{2,1,0:T(8,128)(2,1)}), bf16[1,896,2304]{2,1,0:T(8,128)(2,1)}) %all-gather.36.cloned.1.call-update) | async-done | bytes 4128784 | tf_op jit(solution)/vmap(jvp())/squeeze | solution.py:27
  201.7 26.9 %fusion.82 = f32[4096,2304]{1,0:T(8,128)} fusion(bf16[1,1,4096,896]{2,3,1,0:T(8,128)(2,1)} %get-tuple-element.15, f32[4096]{0:T(1024)S(1)} %bitcast.274, bf16[1,896,2304]{2,1,0:T(8,128)(2,1)} %all-gather.36.cloned.1.call-done), kind=kOutput, calls=%fused_computation.85 | convolution fusion | flops 16922443776 | bytes 49233920 | tf_op jit(solution)/vmap(jvp())/dot_general | solution.py:20
  228.5 20.9 %all-gather.40.cloned.1.call-done = bf16[1,896,2304]{2,1,0:T(8,128)(2,1)} async-done(((bf16[1,56,2304]{2,1,0:T(8,128)(2,1)}), bf16[1,896,2304]{2,1,0:T(8,128)(2,1)}) %all-gather.40.cloned.1.call-update) | async-done | bytes 4128784 | tf_op jit(solution)/vmap(jvp())/squeeze | solution.py:27
  249.4 27.0 %fusion.80 = f32[4096,2304]{1,0:T(8,128)} fusion(bf16[1,1,4096,896]{2,3,1,0:T(8,128)(2,1)} %get-tuple-element.15, f32[4096]{0:T(1024)S(1)} %bitcast.275, bf16[1,896,2304]{2,1,0:T(8,128)(2,1)} %all-gather.40.cloned.1.call-done), kind=kOutput, calls=%fused_computation.84 | convolution fusion | flops 16922443776 | bytes 49233920 | tf_op jit(solution)/vmap(jvp())/dot_general | solution.py:21
  276.4 20.2 %all-gather.38.cloned.1.call-done = bf16[1,2304,896]{2,1,0:T(8,128)(2,1)} async-done(((bf16[1,144,896]{2,1,0:T(8,128)(2,1)}), bf16[1,2304,896]{2,1,0:T(8,128)(2,1)}) %all-gather.38.cloned.1.call-update) | async-done | bytes 4128784 | tf_op jit(solution)/vmap(jvp())/squeeze | solution.py:27
  296.6 26.5 %fusion.24 = bf16[1,1,4096,2304]{3,2,1,0:T(8,128)(2,1)} fusion(bf16[1,4096,896]{2,1,0:T(8,128)(2,1)} %param, bf16[1,2304,896]{2,1,0:T(8,128)(2,1)} %all-gather.38.cloned.1.call-done), kind=kOutput, calls=%fused_computation.43 | convolution fusion | flops 16920870912 | bytes 30343168 | tf_op jit(solution)/vmap(transpose(jvp()))/dot_general | solution.py:9
  323.1 30.9 %fusion.4 = bf16[4096,2304]{1,0:T(8,128)(2,1)S(1)} fusion(f32[4096,2304]{1,0:T(8,128)} %fusion.82, f32[4096,2304]{1,0:T(8,128)} %fusion.80, bf16[1,1,4096,2304]{3,2,1,0:T(8,128)(2,1)} %fusion.24), kind=kLoop, calls=%fused_computation.10 | loop fusion | flops 113246208 | bytes 113246208
  354.0 6.4 copy-done.1
  360.4 19.1 %fusion.87 = bf16[4096,896]{0,1:T(8,128)(2,1)} fusion(bf16[4096,2304]{1,0:T(8,128)(2,1)S(1)} %fusion.4, bf16[1,896,2304]{2,1,0:T(8,128)(2,1)S(1)} %copy-done.10), kind=kOutput, calls=%fused_computation.89 | convolution fusion | flops 16911433728 | bytes 30343168 | tf_op jit(solution)/vmap(transpose(jvp()))/dot_general | solution.py:20
  379.6 35.0 %fusion.40 = (f32[4096]{0:T(1024)S(1)}, bf16[4096,896]{0,1:T(8,128)(2,1)}) fusion(bf16[1,1,4096,896]{2,3,1,0:T(8,128)(2,1)} %get-tuple-element.15, bf16[4096,896]{0,1:T(8,128)(2,1)} %fusion.87, bf16[1,896,2304]{2,1,0:T(8,128)(2,1)} %all-gather.40.cloned.1.call-done, bf16[1,1,4096,2304]{3,2,1,0:T(8,128)(2,1)} %fusion.24, f32[4096,2304]{1,0:T(8,128)} %fusion.82), kind=kOutput, calls=%fused_computation.62 | convolution fusion | flops 16990072832 | bytes 82788352 | tf_op jit(solution)/vmap(transpose(jvp()))/dot_general | solution.py:21
  414.6 9.8 %fusion.45 = bf16[1,1,4096,896]{2,3,1,0:T(8,128)(2,1)S(1)} fusion(bf16[1,1,4096,896]{2,3,1,0:T(8,128)(2,1)} %get-tuple-element.15, bf16[4096,896]{0,1:T(8,128)(2,1)} %get-tuple-element.17, bf16[1,4096,896]{1,2,0:T(8,128)(2,1)} %copy, f32[4096]{0:T(1024)S(1)} %bitcast.273, f32[4096]{0:T(1024)S(1)} %bitcast.276), kind=kLoop, calls=%fused_computation.67 | loop fusion | flops 25690112 | bytes 29392896 | tf_op jit(solution)/vmap(transpose(jvp()))/add_any | solution.py:13
  424.4 2.9 copy-done
  427.3 24.7 %fusion.65 = f32[1,2304,896]{2,1,0:T(8,128)} fusion(bf16[4096,2304]{1,0:T(8,128)(2,1)} %fusion.26, bf16[1,1,4096,896]{2,3,1,0:T(8,128)(2,1)S(1)} %fusion.45), kind=kOutput, calls=%fused_computation.80 | convolution fusion | flops 16911433728 | bytes 34471936 | tf_op jit(solution)/vmap(transpose(jvp()))/dot_general | solution.py:9
  452.1 0.1 reduce-scatter.39.cloned.1.call-start
  452.2 34.6 %fusion.68 = f32[1,2304,896]{2,1,0:T(8,128)} fusion(bf16[1,4096,896]{2,1,0:T(8,128)(2,1)} %param, f32[4096,2304]{1,0:T(8,128)} %fusion.80, f32[4096,2304]{1,0:T(8,128)} %fusion.82), kind=kOutput, calls=%fused_computation.82 | convolution fusion | flops 16968056832 | bytes 91095040 | tf_op jit(solution)/vmap(transpose(jvp()))/dot_general | solution.py:9
  486.8 0.1 reduce-scatter.35.cloned.1.call-start
  486.9 27.2 %fusion.25 = bf16[1,1,4096,2304]{3,2,1,0:T(8,128)(2,1)} fusion(bf16[1,1,4096,896]{2,3,1,0:T(8,128)(2,1)} %copy-done, bf16[1,2304,896]{2,1,0:T(8,128)(2,1)} %all-gather.34.cloned.1.call-done), kind=kOutput, calls=%fused_computation.44 | convolution fusion | flops 16920870912 | bytes 30343168 | tf_op jit(solution)/vmap(transpose(jvp()))/dot_general | solution.py:9
  514.1 37.7 %fusion.7 = bf16[4096,2304]{1,0:T(8,128)(2,1)} fusion(f32[4096,2304]{1,0:T(8,128)} %fusion.97, f32[4096,2304]{1,0:T(8,128)} %fusion.93, bf16[1,1,4096,2304]{3,2,1,0:T(8,128)(2,1)} %fusion.25), kind=kLoop, calls=%fused_computation.13 | loop fusion | flops 113246208 | bytes 113246208
  551.9 28.8 %fusion.59 = f32[1,896,2304]{2,1,0:T(8,128)} fusion(bf16[1,1,4096,2304]{3,2,1,0:T(8,128)(2,1)} %fusion.24, f32[4096,2304]{1,0:T(8,128)} %fusion.82, bf16[1,1,4096,896]{2,3,1,0:T(8,128)(2,1)} %get-tuple-element.15, f32[4096]{0:T(1024)S(1)} %bitcast.277), kind=kOutput, calls=%fused_computation.78 | convolution fusion | flops 16979066880 | bytes 72237056 | tf_op jit(solution)/vmap(transpose(jvp()))/dot_general | solution.py:21
  580.7 0.1 reduce-scatter.37.cloned.1.call-start
  580.8 23.1 %fusion.95 = bf16[4096,896]{0,1:T(8,128)(2,1)} fusion(bf16[4096,2304]{1,0:T(8,128)(2,1)} %fusion.7, bf16[1,896,2304]{2,1,0:T(8,128)(2,1)} %all-gather.30.cloned.1.call-done), kind=kOutput, calls=%fused_computation.97 | convolution fusion | flops 16911433728 | bytes 30343168 | tf_op jit(solution)/vmap(transpose(jvp()))/dot_general | solution.py:20
  603.9 35.2 %fusion.36 = (f32[4096]{0:T(1024)S(1)}, bf16[4096,896]{0,1:T(8,128)(2,1)}) fusion(bf16[1,4096,896]{1,2,0:T(8,128)(2,1)} %copy.1, bf16[4096,896]{0,1:T(8,128)(2,1)} %fusion.95, bf16[1,896,2304]{2,1,0:T(8,128)(2,1)} %all-gather.32.cloned.1.call-done, bf16[1,1,4096,2304]{3,2,1,0:T(8,128)(2,1)} %fusion.25, f32[4096,2304]{1,0:T(8,128)} %fusion.97), kind=kOutput, calls=%fused_computation.58 | convolution fusion | flops 16990072832 | bytes 82788352 | tf_op jit(solution)/vmap(transpose(jvp()))/dot_general | solution.py:21
  639.1 0.7 fusion.110
  639.8 29.1 %fusion.73 = f32[1,896,2304]{2,1,0:T(8,128)} fusion(bf16[1,1,4096,2304]{3,2,1,0:T(8,128)(2,1)} %fusion.25, f32[4096,2304]{1,0:T(8,128)} %fusion.97, bf16[1,4096,896]{1,2,0:T(8,128)(2,1)} %copy.1, f32[4096]{0:T(1024)S(1)} %bitcast.279), kind=kOutput, calls=%fused_computation.83 | convolution fusion | flops 16979066880 | bytes 72237056 | tf_op jit(solution)/vmap(transpose(jvp()))/dot_general | solution.py:21
  668.9 0.1 reduce-scatter.31.cloned.1.call-start
  669.0 24.1 %convolution_bitcast_fusion = f32[1,896,2304]{2,1,0:T(8,128)} fusion(bf16[4096,2304]{1,0:T(8,128)(2,1)} %copy-done.1, bf16[1,1,4096,896]{2,3,1,0:T(8,128)(2,1)} %get-tuple-element.15, f32[4096]{0:T(1024)S(1)} %bitcast.278), kind=kOutput, calls=%fused_computation.81 | convolution fusion | flops 16922443776 | bytes 34488320 | tf_op jit(solution)/vmap(transpose(jvp()))/dot_general | solution.py:20
  693.2 0.1 reduce-scatter.33.cloned.1.call-start
  693.2 24.3 %fusion.62 = f32[1,896,2304]{2,1,0:T(8,128)} fusion(bf16[4096,2304]{1,0:T(8,128)(2,1)} %fusion.7, bf16[1,4096,896]{1,2,0:T(8,128)(2,1)} %copy.1, f32[4096]{0:T(1024)S(1)} %bitcast.280), kind=kOutput, calls=%fused_computation.79 | convolution fusion | flops 16922443776 | bytes 34488320 | tf_op jit(solution)/vmap(transpose(jvp()))/dot_general | solution.py:20
  717.6 12.4 %fusion.44 = bf16[1,4096,896]{1,2,0:T(8,128)(2,1)} fusion(bf16[1,1,4096,896]{2,3,1,0:T(8,128)(2,1)} %copy-done, bf16[4096,896]{0,1:T(8,128)(2,1)} %get-tuple-element.19, bf16[1,4096,896]{1,2,0:T(8,128)(2,1)} %copy.1, f32[4096]{0:T(1024)S(1)} %bitcast.282, f32[4096]{0:T(1024)S(1)} %bitcast.281), kind=kLoop, calls=%fused_computation.66 | loop fusion | flops 25690112 | bytes 29392896 | tf_op jit(solution)/reshape | solution.py:44
  730.0 10.8 %copy.2 = bf16[1,4096,896]{2,1,0:T(8,128)(2,1)} copy(bf16[1,4096,896]{1,2,0:T(8,128)(2,1)} %fusion.44) | data formatting | bytes 14680064
  740.8 1.1 convert_bitcast_fusion
  741.9 1.1 convert_bitcast_fusion.1
  743.0 0.8 add_bitcast_fusion
  743.8 1.1 convert_bitcast_fusion.3
  744.9 34.4 %reduce-scatter.37.cloned.1.call-done = f32[1,56,2304]{2,1,0:T(8,128)} async-done(((f32[1,896,2304]{2,1,0:T(8,128)}), f32[1,56,2304]{2,1,0:T(8,128)}) %reduce-scatter.37.cloned.1.call-update) | async-done | bytes 516112
  779.3 1.1 convert_bitcast_fusion.2
  780.4 0.8 add_bitcast_fusion.1
  781.2 80.6 %reduce-scatter.31.cloned.1.call-done = f32[1,56,2304]{2,1,0:T(8,128)} async-done(((f32[1,896,2304]{2,1,0:T(8,128)}), f32[1,56,2304]{2,1,0:T(8,128)}) %reduce-scatter.31.cloned.1.call-update) | async-done | bytes 516112
  861.8 1.1 convert_bitcast_fusion.5
  862.9 81.3 %reduce-scatter.33.cloned.1.call-done = f32[1,56,2304]{2,1,0:T(8,128)} async-done(((f32[1,896,2304]{2,1,0:T(8,128)}), f32[1,56,2304]{2,1,0:T(8,128)}) %reduce-scatter.33.cloned.1.call-update) | async-done | bytes 516112
  944.2 1.1 convert_bitcast_fusion.4
  945.2 0.8 add_bitcast_fusion.2
  (37 shorter events, 0.8 us)
Async XLA Ops:
  7.2 51.5 %all-gather.30.cloned.1.call-start = ((), (), s32[]{:S(2)}) async-start(), calls=%async_computation.6 | async-start | bytes 4386816 | tf_op jit(solution)/vmap(jvp())/squeeze | solution.py:27
  9.2 97.4 %all-gather.32.cloned.1.call-start = ((), (), s32[]{:S(2)}) async-start(), calls=%async_computation.7 | async-start | bytes 4386816 | tf_op jit(solution)/vmap(jvp())/squeeze | solution.py:27
  11.2 153.7 %all-gather.34.cloned.1.call-start = ((), (), s32[]{:S(2)}) async-start(), calls=%async_computation.8 | async-start | bytes 4386816 | tf_op jit(solution)/vmap(jvp())/squeeze | solution.py:27
  13.3 188.4 %all-gather.36.cloned.1.call-start = ((), (), s32[]{:S(2)}) async-start(), calls=%async_computation.9 | async-start | bytes 4386816 | tf_op jit(solution)/vmap(jvp())/squeeze | solution.py:27
  13.9 235.5 %all-gather.40.cloned.1.call-start = ((), (), s32[]{:S(2)}) async-start(), calls=%async_computation.11 | async-start | bytes 4386816 | tf_op jit(solution)/vmap(jvp())/squeeze | solution.py:27
  14.6 282.0 %all-gather.38.cloned.1.call-start = ((), (), s32[]{:S(2)}) async-start(), calls=%async_computation.10 | async-start | bytes 4386816 | tf_op jit(solution)/vmap(jvp())/squeeze | solution.py:27
  15.2 725.6 %reduce-scatter.41.cloned.1.call-start = ((), (), s32[]{:S(2)}) async-start(), calls=%async_computation.17 | async-start | bytes 8773632
  189.6 0.6 copy-start.2
  190.3 59.2 %copy-start.4 = (f32[1,1,4096]{2,1,0:T(1,128)}, f32[1,1,4096]{2,1,0:T(1,128)S(1)}, u32[]{:S(2)}) copy-start(f32[1,1,4096]{2,1,0:T(1,128)S(1)} %rsqrt.23) | copy-start | bytes 49156
  323.1 37.3 %copy-start.10 = (bf16[1,896,2304]{2,1,0:T(8,128)(2,1)S(1)}, bf16[1,896,2304]{2,1,0:T(8,128)(2,1)}, u32[]{:S(2)}) copy-start(bf16[1,896,2304]{2,1,0:T(8,128)(2,1)} %all-gather.36.cloned.1.call-done) | copy-start | bytes 12386308
  354.0 6.4 copy-start.1
  379.6 35.0 %copy-start.3 = (f32[4096]{0:T(1024)S(1)}, f32[4096]{0:T(1024)}, u32[]{:S(2)}) copy-start(f32[4096]{0:T(1024)} %copy-done.2) | copy-start | bytes 49156
  379.6 35.0 %copy-start.5 = (f32[1,1,4096]{2,1,0:T(1,128)S(1)}, f32[1,1,4096]{2,1,0:T(1,128)}, u32[]{:S(2)}) copy-start(f32[1,1,4096]{2,1,0:T(1,128)} %copy-done.4) | copy-start | bytes 49156
  424.4 2.9 copy-start
  452.1 289.8 %reduce-scatter.39.cloned.1.call-start = ((), (), s32[]{:S(2)}) async-start(), calls=%async_computation.16 | async-start | bytes 8773632
  486.8 257.0 %reduce-scatter.35.cloned.1.call-start = ((), (), s32[]{:S(2)}) async-start(), calls=%async_computation.14 | async-start | bytes 8773632
  514.1 37.7 %copy-start.6 = (f32[1,1,4096]{2,1,0:T(1,128)S(1)}, f32[1,1,4096]{2,1,0:T(1,128)}, u32[]{:S(2)}) copy-start(f32[1,1,4096]{2,1,0:T(1,128)} %copy-done.4) | copy-start | bytes 49156
  580.7 198.6 %reduce-scatter.37.cloned.1.call-start = ((), (), s32[]{:S(2)}) async-start(), calls=%async_computation.15 | async-start | bytes 8773632
  603.9 35.2 %copy-start.9 = (f32[4096]{0:T(1024)S(1)}, f32[4096]{0:T(1024)}, u32[]{:S(2)}) copy-start(f32[4096]{0:T(1024)} %get-tuple-element.12) | copy-start | bytes 49156
  639.8 29.2 %copy-start.7 = (f32[1,1,4096]{2,1,0:T(1,128)S(1)}, f32[1,1,4096]{2,1,0:T(1,128)}, u32[]{:S(2)}) copy-start(f32[1,1,4096]{2,1,0:T(1,128)} %copy-done.4) | copy-start | bytes 49156
  668.9 192.9 %reduce-scatter.31.cloned.1.call-start = ((), (), s32[]{:S(2)}) async-start(), calls=%async_computation.12 | async-start | bytes 8773632
  693.2 24.5 %copy-start.8 = (f32[1,1,4096]{2,1,0:T(1,128)S(1)}, f32[1,1,4096]{2,1,0:T(1,128)}, u32[]{:S(2)}) copy-start(f32[1,1,4096]{2,1,0:T(1,128)} %get-tuple-element.11) | copy-start | bytes 49156
  693.2 251.0 %reduce-scatter.33.cloned.1.call-start = ((), (), s32[]{:S(2)}) async-start(), calls=%async_computation.13 | async-start | bytes 8773632
Sparse Core Ops, SparseCore 0:
  10.0 48.6 all-gather.29
  61.3 45.2 all-gather.31
  108.6 45.2 all-gather.33
  156.3 45.2 all-gather.35
  204.1 45.2 all-gather.39
  251.3 45.2 all-gather.37
  452.2 79.2 reduce-scatter.40
  534.7 79.4 reduce-scatter.38
  617.4 79.2 reduce-scatter.34
  699.8 79.4 reduce-scatter.36
  782.6 79.2 reduce-scatter.30
  864.9 79.1 reduce-scatter.32
where the time goes:
time: 963 us; the launch traced here: 953 us
  matrix products  464 us (48%)
  waiting for transfers between devices  289 us (30%)
  other arithmetic  137 us (14%)
  local copies, waits for them, and re-layouts  48.1 us (5%)
  between operations  14.6 us (2%)
    unnamed x18, waiting for transfers between devices  198 us
    dot_general x6, matrix products, layer(): up = jnp.dot(a, w['w_up'], preferred_element_type=jnp.float32)  182 us
    dot_general x6, matrix products, layer(): gate = jnp.dot(a, w['w_gate'], preferred_element_type=jnp.float32)  144 us
    dot_general x5, matrix products, matmul(): jnp.dot(a, w, preferred_element_type=jnp.float32).astype(jnp.bfloat16)  138 us
    unnamed x3, other arithmetic  100 us
    squeeze x6, waiting for transfers between devices, stack(): h = layer(h, {name: w[number] for name, w in weights.items()})  90.1 us
    unnamed x25, local copies, waits for them, and re-layouts  42.3 us
  transfers between devices with their start and end apart: 12, of which 8 were waited for; matrix products, arithmetic and copies ran while one was open for 51% of the time, Pallas kernels for 0%

commit v1 on v0

v1 whole, which is shorter than its diff:
```python
import functools
import math

import jax
import jax.numpy as jnp
from jax import lax
from jax.experimental import pallas as pl
from jax.experimental.pallas import tpu as pltpu
from jax.sharding import PartitionSpec as P

F32, BF16 = jnp.float32, jnp.bfloat16
ANY = pl.ANY
LIMIT = 64 * 1024 * 1024
NT = (((1,), (1,)), ((), ()))


def dot(a, b):
    return jnp.dot(a, b, preferred_element_type=F32)


def dot_nt(a, b):
    return lax.dot_general(a, b, NT, preferred_element_type=F32)


class Gather:
    def __init__(self, n, layer, shards, outs, sems):
        self.n, self.layer, self.shards, self.outs = n, layer, shards, outs
        self.send, self.recv, self.local = sems
        side = math.isqrt(n)
        self.side = side
        rep, dp = lax.axis_index("rep"), lax.axis_index("dp")
        self.core = lax.rem(rep, 2)
        self.rep, self.partner = rep, rep + 1 - 2 * self.core
        self.i, self.j = dp // side, lax.rem(dp, side)
        self.dp = dp

    @staticmethod
    def sems(n, matrices):
        side = math.isqrt(n)
        k = matrices * (4 + 4 * side + n - 1)
        return [pltpu.SemaphoreType.DMA((k,)), pltpu.SemaphoreType.DMA((k,)), pltpu.SemaphoreType.DMA((matrices,))]

    def at(self, a, b):
        s, c = self.side, self.core
        i = lax.rem(self.i + c * a + (1 - c) * b + 2 * s, s)
        j = lax.rem(self.j + (1 - c) * a + c * b + 2 * s, s)
        return i * s + j

    def piece(self, m, block, core, part=None, shard=False):
        rows = self.shards[m].shape[1]
        cols = self.shards[m].shape[2]
        if cols % 256 == 0:
            col, wide = pl.multiple_of(core * (cols // 2), 128), cols // 2
            first, high = 0, rows
        else:
            col, wide = 0, cols
            first, high = core * (rows // 2), rows // 2
        cut = (high // 2 + 7) // 8 * 8
        if part is not None:
            first, high = (first, cut) if part == 0 else (first + cut, high - cut)
        if shard:
            return self.shards[m].at[self.layer, pl.ds(pl.multiple_of(first, 8), high), pl.ds(col, wide)]
        return self.outs[m].at[pl.ds(pl.multiple_of(block * rows + first, 8), high), pl.ds(col, wide)]

    def copy(self, slot, src, dst, dp, rep=None):
        rep = self.rep if rep is None else rep
        return pltpu.make_async_remote_copy(
            src_ref=src, dst_ref=dst, send_sem=self.send.at[slot], recv_sem=self.recv.at[slot],
            device_id=(rep, dp), device_id_type=pl.DeviceIdType.MESH)

    def each(self, kind, a=0, b=0):
        s = self.side
        out = []
        for m in range(len(self.shards)):
            base = m * (4 + 4 * s + self.n - 1)
            for k, d in enumerate((1, -1)):
                if kind == "first":
                    out.append((base + k, self.piece(m, self.dp, self.core, shard=True), self.piece(m, self.dp, self.core),
                                self.at(d, 0), self.piece(m, self.at(-d, 0), self.core)))
                if kind == "first_on":
                    block = self.piece(m, self.at(-d, 0), self.core, k)
                    out.append((base + 2 + k, block, block, self.at(d, 0), self.piece(m, self.at(2, 0), self.core, k)))
                if kind == "second":
                    block = self.piece(m, self.at(a, 0), self.core)
                    src = self.piece(m, self.dp, self.core, shard=True) if a == 0 else block
                    out.append((base + 4 + 2 * a + k, src, block, self.at(0, d), self.piece(m, self.at(a, -d), self.core)))
                if kind == "second_on":
                    block = self.piece(m, self.at(a, -d), self.core, k)
                    out.append((base + 4 + 2 * s + 2 * a + k, block, block, self.at(0, d), self.piece(m, self.at(a, 2), self.core, k)))
            if kind == "pair":
                block = self.piece(m, self.at(a, b), self.core)
                out.append((base + 4 + 4 * s + a * s + b - 1, block, block, None, self.piece(m, self.at(b, a), 1 - self.core)))
        return out

    def target(self, dp):
        return (dp, None) if dp is not None else (self.dp, self.partner)

    def start(self, *kinds):
        for kind in kinds:
            for slot, src, dst, dp, _ in self.each(*kind):
                self.copy(slot, src, dst, *self.target(dp)).start()

    def arrived(self, *kinds):
        for kind in kinds:
            for slot, _, _, dp, here in self.each(*kind):
                self.copy(slot, here, here, *self.target(dp)).wait_recv()

    def sent(self, *kinds):
        for kind in kinds:
            for slot, src, dst, dp, _ in self.each(*kind):
                self.copy(slot, src, dst, *self.target(dp)).wait_send()

    def own(self):
        out = []
        for m in range(len(self.shards)):
            rows = self.shards[m].shape[1]
            out.append(pltpu.make_async_copy(self.shards[m].at[self.layer],
                                             self.outs[m].at[pl.ds(pl.multiple_of(self.dp * rows, 8), rows)], self.local.at[m]))
        return out

    def stages(self):
        s = self.side
        pairs = [("pair", a, b) for a in range(s) for b in range(s) if a or b]
        ahead = [("first",), ("first_on",)] + [(kind, a) for kind in ("second", "second_on") for a in range(s)]

        def begin():
            barrier = pltpu.get_barrier_semaphore()
            for a, b in ((1, 0), (-1, 0), (0, 1), (0, -1)):
                pl.semaphore_signal(barrier, inc=1, device_id=(self.rep, self.at(a, b)), device_id_type=pl.DeviceIdType.MESH)
            pl.semaphore_signal(barrier, inc=1, device_id=(self.partner, self.dp), device_id_type=pl.DeviceIdType.MESH)
            pl.semaphore_wait(barrier, 5)
            self.start(("first",), ("second", 0))
            for c in self.own():
                c.start()

        def end():
            self.arrived(*pairs)
            self.sent(*ahead, *pairs)
            for c in self.own():
                c.wait()

        def stage(here, on):
            def run():
                self.arrived(*here)
                self.start(*on)
            return run

        near = (1, s - 1)
        return [
            begin,
            stage([("first",)], [("first_on",)] + [("second", a) for a in near] + [("pair", a, 0) for a in near]),
            stage([("second", 0)], [("second_on", 0)] + [("pair", 0, b) for b in near]),
            stage([("first_on",)], [("second", 2), ("pair", 2, 0)]),
            stage([("second", a) for a in near], [("second_on", a) for a in near] + [("pair", a, b) for a in near for b in near]),
            stage([("second_on", 0)], [("pair", 0, 2)]),
            stage([("second", 2)], [("second_on", 2)] + [("pair", 2, b) for b in near]),
            stage([("second_on", a) for a in near], [("pair", a, 2) for a in near]),
            stage([("second_on", 2)], [("pair", 2, 2)]),
            end]


def gathered(shards, n):
    return [jax.ShapeDtypeStruct((w.shape[1] * n, w.shape[2]), w.dtype) for w in shards]


def gather(n, layer, shards):
    M = len(shards)

    def kernel(*refs):
        for stage in Gather(n, layer, refs[:M], refs[M:2 * M], refs[2 * M:]).stages():
            stage()

    return pl.pallas_call(
        kernel, out_shape=gathered(shards, n), in_specs=[pl.BlockSpec(memory_space=ANY)] * M,
        out_specs=[pl.BlockSpec(memory_space=ANY)] * M, scratch_shapes=Gather.sems(n, M), name="gather",
        compiler_params=pltpu.CompilerParams(collective_id=1, has_side_effects=True))(*shards)


class Reduce:
    def __init__(self, n, terms, outs, buffers, sems, greet=True):
        self.n, self.terms, self.outs, self.buffers, self.greet = n, terms, outs, buffers, greet
        self.send, self.recv, self.local = sems
        self.place = Gather.__new__(Gather)
        side = math.isqrt(n)
        rep, dp = lax.axis_index("rep"), lax.axis_index("dp")
        p = self.place
        p.side, p.core, p.rep, p.dp, p.i, p.j = side, lax.rem(rep, 2), rep, dp, dp // side, lax.rem(dp, side)
        self.at, self.rep, self.side = p.at, rep, side

    @staticmethod
    def part_shape(shape, n):
        rows, cols = shape[0] // n, shape[1]
        return (rows, cols // 2) if cols % 256 == 0 else (rows // 2, cols)

    @staticmethod
    def scratch(shapes, n):
        side = math.isqrt(n)
        out = []
        for shape in shapes:
            p = Reduce.part_shape(shape, n)
            out += [pltpu.VMEM(lead + p, BF16) for lead in
                    ((2, side), (2, side), (2, 2, side), (2, side), (2,), (2,), (2, 2), (2, 2))]
        k = len(shapes)
        return out + [pltpu.SemaphoreType.DMA((k * (6 * side + 4),)), pltpu.SemaphoreType.DMA((k * (6 * side + 4),)),
                      pltpu.SemaphoreType.DMA((k * 4 * side,))]

    def term(self, m, block, part):
        rows, cols = self.terms[m].shape[0] // self.n, self.terms[m].shape[1]
        first = block * rows
        high, wide = self.part_shape(self.terms[m].shape, self.n)
        if wide == cols:
            return self.terms[m].at[pl.ds(pl.multiple_of(first + part * high, 8), high)]
        return self.terms[m].at[pl.ds(pl.multiple_of(first, 8), high), pl.ds(part * wide, wide)]

    def copies(self, what):
        s = self.side
        out = []
        for m in range(len(self.terms)):
            r1, own1, r2, own2, s3, r3, s4, r4 = self.buffers[8 * m:8 * m + 8]
            base = m * (6 * s + 4)
            for k, d in enumerate((1, -1)):
                first, second = self.at(d, 0), self.at(0, d)
                for b in range(s):
                    if what == "far":
                        out.append((base + k * s + b, self.term(m, self.at(2, b), k), r1.at[k, b], first))
                    if what == "raw":
                        out.append((base + 2 * s + k * s + b, self.term(m, self.at(d, b), 1 - k), r2.at[k, 1 - k, b], first))
                    if what == "near":
                        out.append((base + 4 * s + k * s + b, r1.at[k, b], r2.at[k, k, b], first))
                if what == "far2":
                    out.append((base + 6 * s + k, s3.at[k], r3.at[k], second))
                if what == "near2":
                    out.append((base + 6 * s + 2 + k, s4.at[k], r4.at[k], second))
        return [pltpu.make_async_remote_copy(src_ref=src, dst_ref=dst, send_sem=self.send.at[i], recv_sem=self.recv.at[i],
                                             device_id=(self.rep, dp), device_id_type=pl.DeviceIdType.MESH)
                for i, src, dst, dp in out]

    def own(self):
        s = self.side
        out = []
        for m in range(len(self.terms)):
            _, own1, _, own2 = self.buffers[8 * m:8 * m + 4]
            for k, d in enumerate((1, -1)):
                for b in range(s):
                    out.append((self.term(m, self.at(d, b), k), own1.at[k, b]))
                    out.append((self.term(m, self.at(0, b), k), own2.at[k, b]))
        return [pltpu.make_async_copy(src, dst, self.local.at[i]) for i, (src, dst) in enumerate(out)]

    def stages(self):
        s, M = self.side, len(self.terms)

        def total(m, part, b):
            _, _, r2, own2 = self.buffers[8 * m:8 * m + 4]
            return own2[part, b].astype(F32) + r2[0, part, b].astype(F32) + r2[1, part, b].astype(F32)

        def begin():
            if self.greet:
                barrier = pltpu.get_barrier_semaphore()
                for a, b in ((1, 0), (-1, 0), (0, 1), (0, -1)):
                    pl.semaphore_signal(barrier, inc=1, device_id=(self.rep, self.at(a, b)), device_id_type=pl.DeviceIdType.MESH)
                pl.semaphore_wait(barrier, 4)
            for c in self.copies("far") + self.copies("raw") + self.own():
                c.start()

        def one():
            for c in self.own():
                c.wait()
            for c in self.copies("far"):
                c.wait_recv()
            for m in range(M):
                r1, own1 = self.buffers[8 * m:8 * m + 2]
                for k in range(2):
                    for b in range(s):
                        r1[k, b] = (r1[k, b].astype(F32) + own1[k, b].astype(F32)).astype(BF16)
            for c in self.copies("near"):
                c.start()

        def two():
            for c in self.copies("raw") + self.copies("near"):
                c.wait_recv()
            for m in range(M):
                s3 = self.buffers[8 * m + 4]
                for k in range(2):
                    s3[k] = total(m, k, 2).astype(BF16)
            for c in self.copies("far2"):
                c.start()

        def three():
            for c in self.copies("far2"):
                c.wait_recv()
            for m in range(M):
                r3, s4 = self.buffers[8 * m + 5:8 * m + 7]
                for k, b in enumerate((1, s - 1)):
                    s4[k, k] = (total(m, k, b) + r3[k].astype(F32)).astype(BF16)
                    s4[k, 1 - k] = total(m, 1 - k, b).astype(BF16)
            for c in self.copies("near2"):
                c.start()

        def four():
            for c in self.copies("near2"):
                c.wait_recv()
            for m in range(M):
                r4 = self.buffers[8 * m + 7]
                high, wide = self.part_shape(self.terms[m].shape, self.n)
                for part in range(2):
                    block = (total(m, part, 0) + r4[0, part].astype(F32) + r4[1, part].astype(F32)).astype(BF16)
                    if wide == self.terms[m].shape[1]:
                        self.outs[m][part * high:(part + 1) * high, :] = block
                    else:
                        self.outs[m][:, part * wide:(part + 1) * wide] = block
            for kind in ("far", "raw", "near", "far2", "near2"):
                for c in self.copies(kind):
                    c.wait_send()

        return [begin, one, two, three, four]


def reduced(terms, n):
    return [jax.ShapeDtypeStruct((t.shape[0] // n, t.shape[1]), BF16) for t in terms]


def spread(stages, when):
    for at, stage in zip(when, stages):
        pl.when(pl.program_id(0) == at)(stage)


def scaled(h):
    wide = h.astype(F32)
    scale = lax.rsqrt(jnp.mean(wide * wide, -1, keepdims=True) + 1e-6)
    return wide, scale, (wide * scale).astype(BF16)


def whole(shape):
    return pl.BlockSpec(shape, lambda i: (0,) * len(shape), pipeline_mode=pl.Buffered(1))


def forward(n, x, wg, wu, wd, shards, tile, step):
    tokens, d = x.shape
    ff = wg.shape[1]
    M = len(shards)
    tiles = tokens // tile
    when = [round(f * (tiles - 1) / 7) for f in (0, 1, 1, 2, 3, 3, 4, 4, 5, 7)]

    def kernel(x_ref, wg_ref, wu_ref, wd_ref, *refs):
        y_ref, gate_ref, up_ref = refs[M:M + 3]
        g = Gather(n, 1, refs[:M], refs[M + 3:2 * M + 3], refs[2 * M + 3:])
        stages = g.stages()
        for at, stage in list(zip(when, stages))[:-1]:
            pl.when(pl.program_id(0) == at)(stage)
        h = x_ref[...]
        _, _, a = scaled(h)
        total = jnp.zeros((tile, d), F32)
        for c in range(0, ff, step):
            gate, up = dot(a, wg_ref[:, c:c + step]), dot(a, wu_ref[:, c:c + step])
            gate_ref[:, c:c + step], up_ref[:, c:c + step] = gate, up
            p = (gate * jax.nn.sigmoid(gate) * up).astype(BF16)
            total += dot(p, wd_ref[c:c + step, :])
        y_ref[...] = h + total.astype(BF16)
        pl.when(pl.program_id(0) == when[-1])(stages[-1])

    rows, broad = pl.BlockSpec((tile, d), lambda i: (i, 0)), pl.BlockSpec((tile, ff), lambda i: (i, 0))
    return pl.pallas_call(
        kernel, grid=(tiles,),
        out_shape=[jax.ShapeDtypeStruct(x.shape, BF16)] + [jax.ShapeDtypeStruct((tokens, ff), F32)] * 2 + gathered(shards, n),
        in_specs=[rows, whole(wg.shape), whole(wu.shape), whole(wd.shape)] + [pl.BlockSpec(memory_space=ANY)] * M,
        out_specs=[rows, broad, broad] + [pl.BlockSpec(memory_space=ANY)] * M, scratch_shapes=Gather.sems(n, M), name="forward",
        cost_estimate=pl.CostEstimate(flops=6 * tokens * d * ff, bytes_accessed=4 * tokens * d + 6 * d * ff, transcendentals=0),
        compiler_params=pltpu.CompilerParams(collective_id=2, has_side_effects=True, vmem_limit_bytes=LIMIT))(x, wg, wu, wd, *shards)


def hidden(gate, up, do, wd, part):
    dp = dot_nt(do, wd[part, :]).astype(BF16).astype(F32)
    sig = jax.nn.sigmoid(gate)
    silu = gate * sig
    return (silu * up).astype(BF16), (dp * up * (sig * (1 + gate * (1 - sig)))).astype(BF16), (dp * silu).astype(BF16)


def through_norm(do, wide, scale, da_g, da_u):
    da = (da_g.astype(BF16) + da_u.astype(BF16)).astype(F32)
    by_scale = jnp.sum(da * wide, -1, keepdims=True)
    by_square = (-1.0 / wide.shape[-1]) * by_scale * (scale * scale * scale)
    return do + (da * scale + wide * by_square).astype(BF16)


def put_out(pairs, stage, sem):
    copies = []
    for k, (piece, out) in enumerate(pairs):
        if k >= 2:
            copies[k - 2].wait()
        stage[k % 2] = piece()
        copies.append(pltpu.make_async_copy(stage.at[k % 2], out, sem.at[k % 2]))
        copies[k].start()
    for c in copies[-2:]:
        c.wait()


def flats(total, out, step):
    def piece(k):
        return lambda: total[:, k * step:(k + 1) * step].astype(BF16).T
    return [(piece(k), out.at[pl.ds(k * step, step)]) for k in range(total.shape[1] // step)]


def plains(total, out, step):
    def piece(k):
        return lambda: total[:, k * step:(k + 1) * step].astype(BF16)
    return [(piece(k), out.at[:, pl.ds(k * step, step)]) for k in range(total.shape[1] // step)]


def backward_last(h, dout, wg, wu, wd, tile, step):
    tokens, d = h.shape
    ff = wg.shape[1]
    tiles = tokens // tile

    def kernel(h_ref, do_ref, wg_ref, wu_ref, wd_ref, dh_ref, dwd_out, dwg_out, dwu_out, dwd, dwg, dwu, stage, flat, sem):
        i = pl.program_id(0)

        @pl.when(i == 0)
        def _():
            for total in (dwd, dwg, dwu):
                total[...] = jnp.zeros_like(total)

        do = do_ref[...]
        wide, scale, a = scaled(h_ref[...])
        do_t, a_t = do.T, a.T
        da_g = jnp.zeros((tile, d), F32)
        da_u = jnp.zeros((tile, d), F32)
        for c in range(0, ff, step):
            part = slice(c, c + step)
            p, dg, du = hidden(dot(a, wg_ref[:, part]), dot(a, wu_ref[:, part]), do, wd_ref, part)
            da_g += dot_nt(dg, wg_ref[:, part])
            da_u += dot_nt(du, wu_ref[:, part])
            dwd[:, part] += dot(do_t, p)
            dwg[:, part] += dot(a_t, dg)
            dwu[:, part] += dot(a_t, du)
        dh_ref[...] = through_norm(do, wide, scale, da_g, da_u)

        @pl.when(i == tiles - 1)
        def _():
            put_out(flats(dwd, dwd_out, step), flat, sem)
            put_out(plains(dwg, dwg_out, step) + plains(dwu, dwu_out, step), stage, sem)

    rows = pl.BlockSpec((tile, d), lambda i: (i, 0))
    any_ = pl.BlockSpec(memory_space=ANY)
    return pl.pallas_call(
        kernel, grid=(tiles,), out_shape=[jax.ShapeDtypeStruct(s, BF16) for s in (h.shape, wd.shape, wg.shape, wu.shape)],
        in_specs=[rows, rows, whole(wg.shape), whole(wu.shape), whole(wd.shape)], out_specs=[rows, any_, any_, any_],
        scratch_shapes=[pltpu.VMEM((d, ff), F32)] * 3
        + [pltpu.VMEM((2, d, step), BF16), pltpu.VMEM((2, step, d), BF16), pltpu.SemaphoreType.DMA((2,))],
        name="backward_last",
        cost_estimate=pl.CostEstimate(flops=16 * tokens * d * ff, bytes_accessed=8 * tokens * d + 12 * d * ff, transcendentals=0),
        compiler_params=pltpu.CompilerParams(vmem_limit_bytes=LIMIT))(h, dout, wg, wu, wd)


def reducing(kernel, n, terms, cid, name, grid, args, in_specs, outs, out_specs, scratch, flops):
    A, O, S, M = len(args), len(outs), len(scratch), len(terms)

    def body(*refs):
        at = [0]

        def take(k):
            at[0] += k
            return refs[at[0] - k:at[0]]

        ins, given, results, sums, own = take(A), take(M), take(O), take(M), take(S)
        rest = refs[at[0]:]
        kernel(ins, results, own, Reduce(n, given, sums, rest[:-3], rest[-3:]).stages())

    out = reduced(terms, n)
    return pl.pallas_call(
        body, grid=grid, out_shape=outs + out, in_specs=in_specs + [pl.BlockSpec(memory_space=ANY)] * M,
        out_specs=out_specs + [whole(o.shape) for o in out], scratch_shapes=scratch + Reduce.scratch([t.shape for t in terms], n),
        name=name, cost_estimate=pl.CostEstimate(flops=flops, bytes_accessed=flops // 1000, transcendentals=0),
        compiler_params=pltpu.CompilerParams(collective_id=cid, has_side_effects=True, vmem_limit_bytes=LIMIT))(*args, *terms)


def backward_hidden(n, h, dout, gate, up, wd, terms, tile, step):
    tokens, d = h.shape
    ff = wd.shape[0]
    tiles = tokens // tile
    when = [round(f * (tiles - 1)) for f in (0, 0.47, 0.74, 0.87, 1)]

    def kernel(ins, results, own, stages):
        h_ref, do_ref, gate_ref, up_ref, wd_ref = ins
        dwd_out, at_ref, dg_ref, du_ref = results
        dwd, flat, sem = own
        i = pl.program_id(0)
        spread(stages[:-1], when[:-1])

        @pl.when(i == 0)
        def _():
            dwd[...] = jnp.zeros_like(dwd)

        do = do_ref[...]
        _, _, a = scaled(h_ref[...])
        do_t = do.T
        at_ref[...] = a.T
        for c in range(0, ff, step):
            part = slice(c, c + step)
            p, dg_ref[:, part], du_ref[:, part] = hidden(gate_ref[:, part], up_ref[:, part], do, wd_ref, part)
            dwd[:, part] += dot(do_t, p)

        @pl.when(i == tiles - 1)
        def _():
            put_out(flats(dwd, dwd_out, step), flat, sem)

        spread(stages[-1:], when[-1:])

    rows = pl.BlockSpec((tile, d), lambda i: (i, 0))
    broad = pl.BlockSpec((tile, ff), lambda i: (i, 0))
    shapes = [(ff, d), (d, tokens), (tokens, ff), (tokens, ff)]
    return reducing(
        kernel, n, terms, 3, "backward_hidden", (tiles,), (h, dout, gate, up, wd),
        [rows, rows, broad, broad, whole(wd.shape)], [jax.ShapeDtypeStruct(s, BF16) for s in shapes],
        [pl.BlockSpec(memory_space=ANY), pl.BlockSpec((d, tile), lambda i: (0, i)), broad, broad],
        [pltpu.VMEM((d, ff), F32), pltpu.VMEM((2, step, d), BF16), pltpu.SemaphoreType.DMA((2,))], 4 * tokens * d * ff)


def backward_tail(n, h, dout, a_t, dg, du, wg, wu, older, dwd, tile, step):
    tokens, d = h.shape
    ff = dg.shape[1]
    half, tiles = ff // step, tokens // tile
    full = 2 * half
    late = tiles / 16
    whens = [[round(f * half / 9) for f in (0, 5, 9, 11, 14)],
             [round(f * half / 9) for f in (3, 9, 13, 15, 17)],
             [round(f * half / 9) for f in (9, 16)] + [full + round(f * late) for f in (2, 4, 6)],
             [full + round(f * late) for f in (0, 5, 9, 11, 13)]]
    terms = (older, dwd, *[jax.ShapeDtypeStruct((d, ff), BF16)] * 2)
    out = reduced(terms, n)

    def kernel(h_ref, do_ref, dg_ref, du_ref, wg_ref, wu_ref, at_ref, dgc_ref, duc_ref, older_ref, dwd_ref,
               dx_ref, dwg_ref, dwu_ref, *refs):
        sums, (stage, sem), rest = refs[:4], refs[4:6], refs[6:]
        i = pl.program_id(0)

        def place(ref, k):
            return pltpu.make_async_copy(stage, ref.at[:, pl.ds(pl.multiple_of(k * step, 128), step)], sem)

        @pl.when((i >= 1) & (i <= half))
        def _():
            place(dwg_ref, i - 1).wait()

        @pl.when((i >= half + 1) & (i <= full))
        def _():
            place(dwu_ref, i - 1 - half).wait()

        for k, ref in enumerate((older_ref, dwd_ref, dwg_ref, dwu_ref)):
            spread(Reduce(n, [ref], [sums[k]], rest[11 * k:11 * k + 8], rest[11 * k + 8:11 * k + 11], k == 0).stages(), whens[k])

        @pl.when(i < half)
        def _():
            stage[...] = dot(at_ref[...], dgc_ref[...]).astype(BF16)
            place(dwg_ref, i).start()

        @pl.when((i >= half) & (i < full))
        def _():
            stage[...] = dot(at_ref[...], duc_ref[...]).astype(BF16)
            place(dwu_ref, i - half).start()

        @pl.when(i >= full)
        def _():
            wide, scale, _ = scaled(h_ref[...])
            dx_ref[...] = through_norm(do_ref[...], wide, scale, dot_nt(dg_ref[...], wg_ref[...]), dot_nt(du_ref[...], wu_ref[...]))

    row = lambda i: (jnp.maximum(i - full, 0), 0)
    rows, broad = pl.BlockSpec((tile, d), row), pl.BlockSpec((tile, ff), row)
    any_ = pl.BlockSpec(memory_space=ANY)
    scratch = [pltpu.VMEM((d, step), BF16), pltpu.SemaphoreType.DMA]
    for t in terms:
        scratch += Reduce.scratch([t.shape], n)
    dx, _, _, *sums = pl.pallas_call(
        kernel, grid=(full + tiles,), out_shape=[jax.ShapeDtypeStruct(h.shape, BF16), *terms[2:], *out],
        in_specs=[rows, rows, broad, broad, whole(wg.shape), whole(wu.shape), whole(a_t.shape),
                  pl.BlockSpec((tokens, step), lambda i: (0, jnp.minimum(i, half - 1))),
                  pl.BlockSpec((tokens, step), lambda i: (0, jnp.clip(i - half, 0, half - 1))), any_, any_],
        out_specs=[rows, any_, any_] + [whole(o.shape) for o in out], scratch_shapes=scratch, name="backward_tail",
        cost_estimate=pl.CostEstimate(flops=8 * tokens * d * ff, bytes_accessed=8 * tokens * ff, transcendentals=0),
        compiler_params=pltpu.CompilerParams(collective_id=4, has_side_effects=True, vmem_limit_bytes=LIMIT))(
            h, dout, dg, du, wg, wu, a_t, dg, du, older, dwd)
    return dx, *sums


def solution(mesh):
    n = mesh.shape["dp"]
    if math.isqrt(n) ** 2 != n or math.isqrt(n) != 4:
        raise ValueError("not 4 by 4")

    def step(x, dy, wg, wu, wd):
        shape = x.shape
        x, dy = x[0], dy[0]
        shards = (wg, wu, wd)
        w0 = gather(n, 0, shards)
        h1, gate, up, *w1 = forward(n, x, *w0, shards, 512, 768)
        dh, dwd1, dwg1, dwu1 = backward_last(h1, dy, *w1, 512, 768)
        dwd0, a_t, dg, du, dwd1, dwg1 = backward_hidden(n, x, dh, gate, up, w0[2], [dwd1, dwg1], 256, 768)
        dx, dwu1, dwd0, dwg0, dwu0 = backward_tail(n, x, dh, a_t, dg, du, *w0[:2], dwu1, dwd0, 256, 256)
        return (dx.reshape(shape), jnp.stack((dwg0, dwg1)), jnp.stack((dwu0, dwu1)), jnp.stack((dwd0, dwd1)))

    tokens = P(("rep", "dp"), None, None)
    rows = P(None, "dp", None)
    by = P("rep", "dp", None)
    return jax.shard_map(step, mesh=mesh, in_specs=(tokens, tokens, rows, rows, rows), out_specs=(tokens, by, by, by), check_vma=False)
```

time: 963 us -> 530 us (0.55)
  Pallas kernels: 0 us -> 509 us
  matrix products: 464 us -> 0 us
  waiting for transfers between devices: 289 us -> 0 us
  other arithmetic: 137 us -> 4.3 us
  local copies, waits for them, and re-layouts: 48.1 us -> 6.71 us
  between operations: 14.6 us -> 0.9 us
    pallas_call x0 -> x5, Pallas kernels: none -> 509 us  [the longest x1 190 us: backward_last(): pl.pallas_call(kernel, grid=(tiles,), out_shape=[jax.ShapeDtypeStruct(s,...]
    dot_general x17 -> x0, matrix products: 464 us -> none  [the longest x6 182 us: layer(): up = jnp.dot(a, w['w_up'], preferred_element_type=jnp.float32)]
    unnamed x18 -> x0, waiting for transfers between devices: 198 us -> none
    unnamed x3 -> x0, other arithmetic: 100 us -> none
    squeeze x6 -> x0, waiting for transfers between devices: 90.1 us -> none  [stack(): h = layer(h, {name: w[number] for name, w in weights.items()})]
    unnamed x25 -> x1, local copies, waits for them, and re-layouts: 42.3 us -> 6.71 us
    reshape x4 -> x0, other arithmetic: 14.9 us -> none  [the longest x1 12.4 us: step(): by_x.reshape(shape)]
    add_any x1 -> x0, other arithmetic: 9.79 us -> none  [normed(): wide = h.astype(jnp.float32)]
  transfers between devices with their start and end apart: 12 -> 0, of which waited for: 8 -> 0; matrix products, arithmetic and copies ran while one was open for 51% -> 0% of each run, Pallas kernels for 0% -> 0%
where the time goes in v1:
time: 530 us; the launch traced here: 521 us
  Pallas kernels  509 us (96%)
  local copies, waits for them, and re-layouts  6.71 us (1%)
    pallas_call x1, Pallas kernels, backward_last(): pl.pallas_call(kernel, grid=(tiles,), out_shape=[jax.ShapeDtypeStruct(s,...  190 us
    pallas_call x1, Pallas kernels, backward_tail(): pl.pallas_call(kernel, grid=(full + tiles,), out_shape=[jax.ShapeDtypeStr...  128 us
    pallas_call x1, Pallas kernels, forward(): pl.pallas_call(kernel, grid=(tiles,), out_shape=[jax.ShapeDtypeStruct(x.s...  79.5 us
    pallas_call x1, Pallas kernels, reducing(): pl.pallas_call(body, grid=grid, out_shape=outs + out, in_specs=in_specs +...  67.1 us
    pallas_call x1, Pallas kernels, gather(): pl.pallas_call(kernel, out_shape=gathered(shards, n), in_specs=[pl.BlockS...  44.6 us

profile of v1, /device:TPU:98, one launch (start us, length us, event | category | flops | bytes accessed | tf_op | source)
XLA Modules:
  0.0 521.3 jit_solution(13097496967553137478)
XLA Ops:
  0.6 44.6 %gather.1 = (bf16[896,2304]{1,0:T(8,128)(2,1)}, bf16[896,2304]{1,0:T(8,128)(2,1)}, bf16[2304,896]{1,0:T(8,128)(2,1)}) custom-call(bf16[2,56,2304]{2,1,0:T(8,128)(2,1)} %refs_0_.3, bf16[2,56,2304]{2,1,0:T(8,128)(2,1)} %refs_1_.3, bf16[2,144,896]{2,1,0:T(8,128)(2,1)} %refs_2_.3), custom_call_target="tpu_custom_call" | custom-call | tf_op jit(solution)/shard_map/gather/pallas_call | solution.py:173
  45.2 79.5 %forward.1 = (bf16[4096,896]{1,0:T(8,128)(2,1)}, f32[4096,2304]{1,0:T(8,128)}, f32[4096,2304]{1,0:T(8,128)}, bf16[896,2304]{1,0:T(8,128)(2,1)}, bf16[896,2304]{1,0:T(8,128)(2,1)}, /*index=5*/bf16[2304,896]{1,0:T(8,128)(2,1)}) custom-call(bf16[4096,896]{1,0:T(8,128)(2,1)} %bitcast.17, bf16[896,2304]{1,0:T(8,128)(2,1)} %get-tuple-element.28.wg_ref, ...), custom_call_target="tpu_custom_call" | custom-call | flops 50734301184 | bytes 27066368 | tf_op jit(solution)/shard_map/forward/pallas_call | solution.py:362
  124.8 189.9 %backward_last.1 = (bf16[4096,896]{1,0:T(8,128)(2,1)}, bf16[2304,896]{1,0:T(8,128)(2,1)}, bf16[896,2304]{1,0:T(8,128)(2,1)}, bf16[896,2304]{1,0:T(8,128)(2,1)}) custom-call(bf16[4096,896]{1,0:T(8,128)(2,1)} %get-tuple-element.31.h_ref, bf16[4096,896]{1,0:T(8,128)(2,1)} %bitcast.16, bf16[896,2304]{1,0:T(8,128)(2,1)} %get-tuple-element.32.wg_ref, ...), custom_call_target="tpu_custom_call" | custom-call | flops 135291469824 | bytes 54132736 | tf_op jit(solution)/shard_map/backward_last/pallas_call | solution.py:444
  314.7 67.1 %backward_hidden.1 = (bf16[2304,896]{1,0:T(8,128)(2,1)}, bf16[896,4096]{1,0:T(8,128)(2,1)}, bf16[4096,2304]{1,0:T(8,128)(2,1)}, bf16[4096,2304]{1,0:T(8,128)(2,1...) custom-call(bf16[4096,896]{1,0:T(8,128)(2,1)} %bitcast.18, bf16[4096,896]{1,0:T(8,128)(2,1)} %get-tuple-element.35.refs_1_.do_ref, ...), custom_call_target="tpu_custom_call" | custom-call | flops 33822867456 | bytes 33822868 | tf_op jit(solution)/shard_map/backward_hidden/pallas_call | solution.py:469
  381.8 128.2 %backward_tail.1 = (bf16[4096,896]{1,0:T(8,128)(2,1)}, bf16[896,2304]{1,0:T(8,128)(2,1)}, bf16[896,2304]{1,0:T(8,128)(2,1)}, bf16[56,2304]{1,0:T(8,128)(2,1)}, b...) custom-call(bf16[4096,896]{1,0:T(8,128)(2,1)} %bitcast.19, ...), custom_call_target="tpu_custom_call" | custom-call | flops 67645734912 | bytes 75497472 | tf_op jit(solution)/shard_map/backward_tail/pallas_call | solution.py:571
  510.0 2.4 pad_maximum_fusion
  512.4 1.9 pad_maximum_fusion.2
  514.3 6.7 %copy.10 = bf16[1,4096,896]{2,1,0:T(8,128)(2,1)} copy(bf16[1,4096,896]{2,1,0:T(8,128)(2,1)} %bitcast.9) | data formatting | bytes 14680064
